TPU v7x, 64 devices: a 2x2x8 block of a 4x4x8 slice. The times are simulated.
64 devices in a mesh: dp: 4 (over x, y), dcp: 16 (over z, core).
Axes of the slice: x: 2, y: 2, z: 8, core: 2. Of those that a mesh axis runs over, the one named last changes fastest.
The devices are a block of a 4x4x8 slice.
Arguments:
- q: bfloat16 [64, 128, 576], P('dp', 'dcp'), parts along dimension 0
- cache: bfloat16 [64, 128, 16, 8, 576], P('dp', None, 'dcp'), parts along dimension 0
- lens: int32 [64], P('dp'), parts along dimension 0
Outputs:
- output: bfloat16 [64, 128, 512], P('dp', 'dcp'), parts along dimension 0
There are 4 independent parts. A program takes and returns all parts, laid end to end along the dimension named above; each array names one.
All inputs are finite; a program needn't handle non-finite values.
Results may differ from a plain program's by a relative error of at most 0.00646929.
Values are sent between devices in bfloat16 or wider.
A program may use at most 768 MiB of HBM per device.

v0:
```python
import jax
import jax.numpy as jnp
from jax import lax
from jax.sharding import PartitionSpec as P

ROPE = 64
QK_DIM = 192
SCALE = QK_DIM ** -0.5


def solution(mesh):
    n = mesh.shape['dcp']

    def local(q, cache, lens):
        b, hl, k = q.shape
        r = cache.shape[1]
        page = cache.shape[3]
        lorav = k - ROPE
        d = lax.axis_index('dcp')
        qa = lax.all_gather(q, 'dcp', axis=1, tiled=True)
        c = cache.reshape(b, r * page, k)
        pos = (jnp.arange(r)[:, None] * n + d) * page + jnp.arange(page)[None, :]
        valid = pos.reshape(r * page)[None, :] < lens[:, None]
        s = jnp.einsum('bhk,btk->bht', qa, c, preferred_element_type=jnp.float32) * SCALE
        s = jnp.where(valid[:, None, :], s, -jnp.inf)
        m = jnp.max(s, axis=2)
        m = jnp.where(jnp.isfinite(m), m, 0.0)
        p = jnp.exp(s - m[:, :, None])
        l = jnp.sum(p, axis=2)
        has = l > 0.0
        lsafe = jnp.where(has, l, 1.0)
        pv = jnp.einsum('bht,btk->bhk', p.astype(jnp.bfloat16), c[:, :, :lorav], preferred_element_type=jnp.float32)
        od = (pv / lsafe[:, :, None]).astype(jnp.bfloat16)
        lse = jnp.where(has, m + jnp.log(lsafe), -jnp.inf)
        od = lax.all_to_all(od.reshape(b, n, hl, lorav), 'dcp', 1, 1, tiled=True)
        lse = lax.all_to_all(lse.reshape(b, n, hl), 'dcp', 1, 1, tiled=True)
        top = jnp.max(lse, axis=1)
        w = jnp.exp(lse - top[:, None, :])
        o = jnp.sum(w[:, :, :, None] * od.astype(jnp.float32), axis=1) / jnp.sum(w, axis=1)[:, :, None]
        return o.astype(jnp.bfloat16)

    return jax.shard_map(local, mesh=mesh, in_specs=(P('dp', 'dcp', None), P('dp', None, 'dcp', None, None), P('dp')), out_specs=P('dp', 'dcp', None), check_vma=False)
```

profile of v0, /device:TPU:21, one launch (start us, length us, event | category | flops | bytes accessed | tf_op | source)
XLA Modules:
  0.0 150.3 jit_solution(15214140844480384931)
XLA Ops:
  6.6 0.7 all-gather.2.cloned.1.call-update
  7.3 0.1 iota_add_fusion
  7.4 0.1 add.40
  7.5 0.0 copy-start
  7.5 28.0 %copy.11 = bf16[16,128,1,8,576]{4,3,1,0,2:T(8,128)(2,1)} copy(bf16[16,128,1,8,576]{1,4,3,2,0:T(8,128)(2,1)} %param.4) | data formatting | bytes 37748736 | tf_op args[1]
  35.5 0.1 broadcast_compare_fusion
  35.6 15.1 %all-gather.2.cloned.1.call-done = bf16[16,128,576]{2,1,0:T(8,128)(2,1)} async-done(((bf16[16,8,576]{2,1,0:T(8,128)(2,1)}), bf16[16,128,576]{2,1,0:T(8,128)(2,1)}) %all-gather.2.cloned.1.call-update) | async-done | bytes 2359312 | tf_op jit(solution)/shard_map/all_gather | solution.py:20
  50.7 13.9 %fusion.2 = (f32[16,128]{1,0:T(8,128)S(1)}, f32[16,128,1024]{2,1,0:T(8,128)}) fusion(pred[16,1024]{1,0:T(8,128)(4,1)S(1)} %broadcast_compare_fusion, bf16[16,128,576]{2,1,0:T(8,128)(2,1)} %all-gather.2.cloned.1.call-done, bf16[16,128,1,8,576]{4,3,1,0,2:T(8,128)(2,1)} %copy.11), kind=kOutput, calls=%fused_computation.4 | convolution fusion | flops 2422208512 | bytes 29646848 | tf_op jit(solution)/shard_map/bhk,btk->bht/dot_general | solution.py:24
  64.6 0.1 copy.14
  64.7 4.5 %fusion.4 = f32[16,128]{1,0:T(8,128)S(1)} fusion(f32[16,128,1024]{2,1,0:T(8,128)} %get-tuple-element.8, f32[16,128]{1,0:T(8,128)S(1)} %is-finite_select_fusion.1, pred[16,1024]{1,0:T(8,128)(4,1)S(1)} %broadcast_compare_fusion), kind=kLoop, calls=%fused_computation.6 | loop fusion | flops 8386560 | bytes 8421376 | tf_op jit(solution)/shard_map/reduce_sum | solution.py:29
  69.2 0.1 copy.13
  69.4 0.7 reshape.68
  70.1 4.6 %all-to-all-start = ((f32[16,1,128]{2,1,0:T(1,128)}), f32[16,1,128]{2,1,0:T(1,128)S(1)}, u32[]{:S(2)}, u32[]{:S(2)}) async-start(f32[16,1,128]{2,1,0:T(1,128)} %reshape.68), calls=%async_computation | async-start | bytes 16384 | tf_op jit(solution)/shard_map/all_to_all | solution.py:36
  74.7 10.0 %fusion.10 = bf16[16,16,8,512]{3,2,1,0:T(8,128)(2,1)S(1)} fusion(f32[16,128]{1,0:T(8,128)S(1)} %compare_select_fusion.2, bf16[16,1024,576]{2,1,0:T(8,128)(2,1)} %bitcast.21, f32[16,128,1024]{2,1,0:T(8,128)} %get-tuple-element.8, f32[16,128]{1,0:T(8,128)S(1)} %is-finite_select_fusion.1, pred[16,1024]{1,0:T(8,128)(4,1)S(1)} %broadcast_compare_fusion), kind=kOutput, calls=%fused_computation.13 | convolution fusion | flops 2157969408 | bytes 27295744 | tf_op jit(solution)/shard_map/bht,btk->bhk/dot_general | solution.py:32
  84.6 1.6 %copy.16 = bf16[16,16,8,512]{3,2,0,1:T(8,128)(2,1)} copy(bf16[16,16,8,512]{3,2,1,0:T(8,128)(2,1)S(1)} %fusion.10) | data formatting | bytes 4194304 | tf_op jit(solution)/shard_map/reshape | solution.py:35
  86.2 7.2 %all-to-all-start.1 = ((bf16[16,16,8,512]{3,2,0,1:T(8,128)(2,1)}), bf16[16,16,8,512]{3,2,0,1:T(8,128)(2,1)S(1)}, u32[]{:S(2)}, u32[]{:S(2)}) async-start(bf16[16,16,8,512]{3,2,0,1:T(8,128)(2,1)} %copy.16), calls=%async_computation.1 | async-start | bytes 4194304 | tf_op jit(solution)/shard_map/all_to_all | solution.py:35
  93.4 0.5 broadcast.53
  93.9 0.7 reduce
  94.6 0.1 reshape.69
  94.8 0.1 copy.15
  94.8 0.1 copy.17
  94.9 47.3 %all-to-all-done.1 = bf16[16,16,8,512]{3,2,0,1:T(8,128)(2,1)S(1)} async-done(((bf16[16,16,8,512]{3,2,0,1:T(8,128)(2,1)}), bf16[16,16,8,512]{3,2,0,1:T(8,128)(2,1)S(1)}, u32[]{:S(2)}, u32[]{:S(2)}) %all-to-all-start.1) | async-done | bytes 2097184 | tf_op jit(solution)/shard_map/all_to_all | solution.py:35
  142.2 0.5 multiply_reduce_fusion
  142.7 0.7 divide_convert_fusion.1
  (9 shorter events, 0.1 us)
Async XLA Ops:
  6.5 44.2 %all-gather.2.cloned.1.call-start = ((), (), s32[]{:S(2)}) async-start(), calls=%async_computation.2 | async-start | bytes 2785280 | tf_op jit(solution)/shard_map/all_gather | solution.py:20
  7.5 28.0 %copy-start = (s32[16]{0:T(128)S(1)}, s32[16]{0:T(128)}, u32[]{:S(2)}) copy-start(s32[16]{0:T(128)} %param.5) | copy-start | bytes 196
  70.1 16.1 %all-to-all-start = ((f32[16,1,128]{2,1,0:T(1,128)}), f32[16,1,128]{2,1,0:T(1,128)S(1)}, u32[]{:S(2)}, u32[]{:S(2)}) async-start(f32[16,1,128]{2,1,0:T(1,128)} %reshape.68), calls=%async_computation | async-start | bytes 16384 | tf_op jit(solution)/shard_map/all_to_all | solution.py:36
  86.2 56.0 %all-to-all-start.1 = ((bf16[16,16,8,512]{3,2,0,1:T(8,128)(2,1)}), bf16[16,16,8,512]{3,2,0,1:T(8,128)(2,1)S(1)}, u32[]{:S(2)}, u32[]{:S(2)}) async-start(bf16[16,16,8,512]{3,2,0,1:T(8,128)(2,1)} %copy.16), calls=%async_computation.1 | async-start | bytes 4194304 | tf_op jit(solution)/shard_map/all_to_all | solution.py:35
Sparse Core Ops, SparseCore 0:
  8.9 41.7 all-gather.1
where the time goes:
time: 151 us; the launch traced here: 150 us
  waiting for transfers between devices  63.2 us (42%)
  local copies, waits for them, and re-layouts  31.3 us (21%)
  matrix products  23.8 us (16%)
  between operations  13.5 us (9%)
  starting transfers between devices  11.9 us (8%)
  other arithmetic  6.66 us (4%)
    all_to_all x1, waiting for transfers between devices, local(): od = lax.all_to_all(od.reshape(b, n, hl, lorav), 'dcp', 1, 1, tiled=True)  47.3 us
    unnamed x5, local copies, waits for them, and re-layouts  28.8 us
    all_gather x1, waiting for transfers between devices, local(): qa = lax.all_gather(q, 'dcp', axis=1, tiled=True)  15.1 us
    dot_general x1, matrix products, local(): jnp.einsum('bhk,btk->bht', qa, c, preferred_element_type=jnp.float32)  13.9 us
    dot_general x1, matrix products, local(): jnp.einsum('bht,btk->bhk', p.astype(jnp.bfloat16), c[:, :, :lorav], prefe...  9.95 us
    all_to_all x1, starting transfers between devices, local(): od = lax.all_to_all(od.reshape(b, n, hl, lorav), 'dcp', 1, 1, tiled=True)  7.25 us
    all_to_all x1, starting transfers between devices, local(): lse = lax.all_to_all(lse.reshape(b, n, hl), 'dcp', 1, 1, tiled=True)  4.6 us
    reduce_sum x1, other arithmetic, local(): l = jnp.sum(p, axis=2)  4.54 us
  transfers between devices with their start and end apart: 3, of which 2 were waited for; matrix products, arithmetic and copies ran while one was open for 27% of the time, Pallas kernels for 0%

commit v1 on v0

v1 whole, which is shorter than its diff:
```python
import functools
import jax
import jax.numpy as jnp
from jax import lax
from jax.experimental import pallas as pl
from jax.experimental.pallas import tpu as pltpu
from jax.sharding import PartitionSpec as P

ROPE = 64
QK_DIM = 192
SCALE = QK_DIM ** -0.5
NEG = -2.0e38
NB = 2
QB = 4
L2, L3, L4, L5 = 1, 3, 4, 5
MESH = pl.DeviceIdType.MESH
F32 = jnp.float32
BF16 = jnp.bfloat16


def mix(rows):
    top = functools.reduce(jnp.maximum, rows)
    ws = [jnp.exp(x - top) for x in rows]
    tot = functools.reduce(jnp.add, ws)
    inv = 1.0 / tot
    return [w * inv for w in ws], top + jnp.log(tot)


def kernel(n, page, lens_ref, q_ref, c_ref, o_ref,
           qg, cb, of, od, lf, ld, pw, pr, asnd, arcv, alsnd, alrcv, bsnd, brcv, blsnd, blrcv,
           r2s, r2r, r2ls, r2lr, r1s, r1r, r1ls, r1lr,
           csem, qsem, qss, qsr, qds, qdr, ods, odr, lds, ldr,
           ass, asr, alss, alsr, bss, bsr, blss, blsr,
           r2ss, r2sr, r2lss, r2lsr, r1ss, r1sr, r1lss, r1lsr):
    me = lax.axis_index('dcp')
    Z = n // 2
    H = Z // 2
    z = me // 2
    core = me % 2
    other = 1 - core
    peer = 2 * z + other
    nseq, hl, kd = q_ref.shape
    R = c_ref.shape[3]
    T = page * R
    lora = o_ref.shape[2]
    CH = nseq // NB
    CQ = nseq // QB
    DIRS = (1, -1)

    def chip(d):
        return (z + (d + Z)) % Z

    def dev(d):
        return 2 * chip(d) + core

    def remote(src, dst, ss, rs, to):
        return pltpu.make_async_remote_copy(src_ref=src, dst_ref=dst, send_sem=ss, recv_sem=rs,
                                            device_id={'dcp': to}, device_id_type=MESH)

    def mine(dv, lo, cnt):
        return qg.at[pl.ds(lo, cnt), pl.ds(pl.multiple_of(dv * hl, hl), hl), :]

    qcp = pltpu.make_async_copy(q_ref, mine(me, 0, nseq), qsem.at[0])
    qcp.start()

    bar = pltpu.get_barrier_semaphore()
    partners = [peer, dev(1), dev(-1), dev(2), dev(-2)]
    for t in partners:
        pl.semaphore_signal(bar, inc=1, device_id={'dcp': t}, device_id_type=MESH)

    def ccopy(i):
        return pltpu.make_async_copy(c_ref.at[i], cb.at[i], csem.at[i])

    qcp.wait()
    pl.semaphore_wait(bar, len(partners))

    def qring(si, h, c):
        s = DIRS[si]
        blk = mine(dev(-s * h), c * QB, QB)
        return remote(blk, blk, qss.at[si, h, c], qsr.at[si, h, c], dev(s))

    def qd2d(si, h, c):
        s = DIRS[si]
        blk = mine(dev(-s * (h + 1)), c * QB, QB)
        return remote(blk, blk, qds.at[si, h, c], qdr.at[si, h, c], peer)

    def qarrive(si, h, c):
        s = DIRS[si]
        blk = mine(2 * chip(-s * (h + 1)) + other, c * QB, QB)
        return remote(blk, blk, qds.at[si, h, c], qdr.at[si, h, c], peer)

    def qrecv(si, h, c):
        s = DIRS[si]
        blk = mine(dev(-s * (h + 1)), c * QB, QB)
        return remote(blk, blk, qss.at[si, h, c], qsr.at[si, h, c], dev(s))

    def half(si):
        return range(CQ // 2) if si == 0 else range(CQ // 2, CQ)

    sends = []
    own = mine(me, 0, nseq)
    for c in range(CQ):
        for si in range(2):
            x = qring(si, 0, c)
            x.start()
            sends.append(x)
    dself = remote(own, own, qsem.at[1], qsem.at[2], peer)
    dself.start()
    sends.append(dself)

    for i in range(nseq):
        ccopy(i).start()

    for h in range(H):
        for c in range(CQ):
            for si in range(2):
                if h == H - 1 and c not in half(si):
                    continue
                qrecv(si, h, c).wait_recv()
                if h < H - 2 or (h == H - 2 and c in half(si)):
                    x = qring(si, h + 1, c)
                    x.start()
                    sends.append(x)
                x = qd2d(si, h, c)
                x.start()
                sends.append(x)
    pown = mine(peer, 0, nseq)
    remote(pown, pown, qsem.at[1], qsem.at[2], peer).wait_recv()
    for h in range(H):
        for c in range(CQ):
            for si in range(2):
                if h == H - 1 and c not in half(si):
                    continue
                qarrive(si, h, c).wait_recv()

    lane = lax.broadcasted_iota(jnp.int32, (hl, 128), 1)
    sub = lax.broadcasted_iota(jnp.int32, (hl, 128), 0)
    row1 = lax.broadcasted_iota(jnp.int32, (1, 128), 1)
    tt = lax.broadcasted_iota(jnp.int32, (1, T), 1)
    pos = ((tt % R) * n + me) * page + tt // R

    def col(row, j):
        return jnp.sum(jnp.where(lane == j * hl + sub, row, 0.0), axis=1, keepdims=True)

    def d2d_o(k):
        return (remote(of.at[k, :, :, other], od.at[k], ods.at[k], odr.at[k], peer),
                remote(lf.at[k, :, other], ld.at[k], lds.at[k], ldr.at[k], peer))

    def compute(k):
        lses = []
        for j in range(NB):
            b = k * NB + j
            ccopy(b).wait()
            qb = qg[b]
            cc = jnp.concatenate([cb[b, i] for i in range(page)], axis=1)
            s = jnp.dot(qb, cc, preferred_element_type=F32) * SCALE
            s = jnp.where(pos < lens_ref[b], s, NEG)
            m = jnp.max(s, axis=1, keepdims=True)
            m = jnp.where(m > NEG, m, 0.0)
            p = jnp.exp(s - m)
            l = jnp.sum(p, axis=1, keepdims=True)
            has = l > 0.0
            ls = jnp.where(has, l, 1.0)
            vv = jnp.concatenate([cb[b, i, :lora] for i in range(page)], axis=1)
            acc = lax.dot_general(p.astype(BF16), vv, (((1,), (1,)), ((), ())), preferred_element_type=F32)
            acc = acc * (1.0 / ls)
            of[k, j] = acc.reshape(Z, 2, hl, lora)
            lses.append(jnp.where(has, m + jnp.log(ls), NEG))
        x = jnp.zeros((n * hl, 128), F32)
        lane2 = lax.broadcasted_iota(jnp.int32, (n * hl, 128), 1)
        row2 = lax.broadcasted_iota(jnp.int32, (n * hl, 128), 0) % hl
        for j in range(NB):
            x = jnp.where(lane2 == j * hl + row2, lses[j], x)
        x = jnp.sum(x.reshape(n, hl, 128), axis=1, keepdims=True)
        lf[k] = x.reshape(Z, 2, 1, 128)
        for x in d2d_o(k):
            x.start()

    def snd_a(si, k):
        to = dev(2 * DIRS[si])
        return (remote(asnd.at[si, k], arcv.at[si, k], ass.at[si, k], asr.at[si, k], to),
                remote(alsnd.at[si, k], alrcv.at[si, k], alss.at[si, k], alsr.at[si, k], to))

    def snd_b(si, k):
        to = dev(DIRS[si])
        return (remote(bsnd.at[si, k], brcv.at[si, k], bss.at[si, k], bsr.at[si, k], to),
                remote(blsnd.at[si, k], blrcv.at[si, k], blss.at[si, k], blsr.at[si, k], to))

    def snd_2(si, k):
        to = dev(DIRS[si])
        return (remote(r2s.at[si, k], r2r.at[si, k], r2ss.at[si, k], r2sr.at[si, k], to),
                remote(r2ls.at[si, k], r2lr.at[si, k], r2lss.at[si, k], r2lsr.at[si, k], to))

    def snd_1(si, k):
        to = dev(DIRS[si])
        return (remote(r1s.at[si, k], r1r.at[si, k], r1ss.at[si, k], r1sr.at[si, k], to),
                remote(r1ls.at[si, k], r1lr.at[si, k], r1lss.at[si, k], r1lsr.at[si, k], to))

    def stage2(k):
        for x in d2d_o(k):
            x.wait_recv()
        for d in (H, 3, -3, 2, -2, 1, -1, 0):
            t = chip(d)
            (a0, a1), lr = mix([lf[k, t, core], ld[k, t]])
            if d == H:
                for si in range(2):
                    alsnd[si, k] = jnp.where(row1 // hl == si, lr, NEG)
            elif abs(d) == 3:
                blsnd[0 if d > 0 else 1, k] = lr
            else:
                pr[d + 2, k] = lr
            for j in range(NB):
                o = col(a0, j) * of[k, j, t, core] + col(a1, j) * od[k, j, t]
                if d == H:
                    asnd[j, k] = o.astype(BF16)
                elif abs(d) == 3:
                    bsnd[0 if d > 0 else 1, k, j] = o.astype(BF16)
                else:
                    pw[d + 2, k, j] = o
        for si in range(2):
            for x in snd_a(si, k) + snd_b(si, k):
                x.start()

    def stage3(k):
        for si in range(2):
            for x in snd_a(si, k) + snd_b(si, k):
                x.wait_recv()
            d = 2 * DIRS[si]
            (a0, a1, a2), lr = mix([pr[d + 2, k], blrcv[si, k], alrcv[si, k]])
            for j in range(NB):
                o = col(a0, j) * pw[d + 2, k, j] + col(a1, j) * brcv[si, k, j].astype(F32)
                if j == si:
                    o = o + col(a2, j) * arcv[si, k].astype(F32)
                r2s[si, k, j] = o
            r2ls[si, k] = lr
            for x in snd_2(si, k):
                x.start()

    def stage4(k):
        for si in range(2):
            for x in snd_2(si, k):
                x.wait_recv()
            d = DIRS[si]
            (a0, a1), lr = mix([pr[d + 2, k], r2lr[si, k]])
            for j in range(NB):
                r1s[si, k, j] = col(a0, j) * pw[d + 2, k, j] + col(a1, j) * r2r[si, k, j]
            r1ls[si, k] = lr
            for x in snd_1(si, k):
                x.start()

    def stage5(k):
        for si in range(2):
            for x in snd_1(si, k):
                x.wait_recv()
        (a0, a1, a2), _ = mix([pr[2, k], r1lr[0, k], r1lr[1, k]])
        for j in range(NB):
            o = col(a0, j) * pw[2, k, j] + col(a1, j) * r1r[0, k, j] + col(a2, j) * r1r[1, k, j]
            o_ref[k * NB + j] = o.astype(BF16)

    def step(k, carry):
        @pl.when(k < CH)
        def _():
            compute(k)
        for lag, stage in ((L2, stage2), (L3, stage3), (L4, stage4), (L5, stage5)):
            @pl.when((k >= lag) & (k < CH + lag))
            def _(lag=lag, stage=stage):
                stage(k - lag)
        return carry

    lax.fori_loop(0, CH + L5, step, 0)

    for x in sends:
        x.wait_send()

    def drain(k, carry):
        for x in d2d_o(k):
            x.wait_send()
        for si in range(2):
            for x in snd_a(si, k) + snd_b(si, k) + snd_2(si, k) + snd_1(si, k):
                x.wait_send()
        return carry

    lax.fori_loop(0, CH, drain, 0)


def solution(mesh):
    n = mesh.shape['dcp']

    def local(q, cache, lens):
        b, hl, k = q.shape
        r = cache.shape[1]
        page = cache.shape[3]
        lora = k - ROPE
        T = r * page
        c = cache.reshape(b, r, page, k).transpose(0, 2, 3, 1)
        Z = n // 2
        CH = b // NB
        CQ = b // QB
        V = pltpu.VMEM
        D = pltpu.SemaphoreType.DMA
        scratch = [
            V((b, n * hl, k), BF16), V((b, page, k, r), BF16),
            V((CH, NB, Z, 2, hl, lora), F32), V((CH, NB, Z, hl, lora), F32),
            V((CH, Z, 2, 1, 128), F32), V((CH, Z, 1, 128), F32),
            V((5, CH, NB, hl, lora), F32), V((5, CH, 1, 128), F32),
            V((2, CH, hl, lora), BF16), V((2, CH, hl, lora), BF16), V((2, CH, 1, 128), F32), V((2, CH, 1, 128), F32),
            V((2, CH, NB, hl, lora), BF16), V((2, CH, NB, hl, lora), BF16), V((2, CH, 1, 128), F32), V((2, CH, 1, 128), F32),
            V((2, CH, NB, hl, lora), F32), V((2, CH, NB, hl, lora), F32), V((2, CH, 1, 128), F32), V((2, CH, 1, 128), F32),
            V((2, CH, NB, hl, lora), F32), V((2, CH, NB, hl, lora), F32), V((2, CH, 1, 128), F32), V((2, CH, 1, 128), F32),
            D((b,)), D((3,)),
            D((2, Z // 2, CQ)), D((2, Z // 2, CQ)), D((2, Z // 2, CQ)), D((2, Z // 2, CQ)),
            D((CH,)), D((CH,)), D((CH,)), D((CH,)),
        ] + [D((2, CH))] * 16
        return pl.pallas_call(
            functools.partial(kernel, n, page),
            out_shape=jax.ShapeDtypeStruct((b, hl, lora), BF16),
            in_specs=[pl.BlockSpec(memory_space=pltpu.SMEM), pl.BlockSpec(memory_space=pl.ANY),
                      pl.BlockSpec(memory_space=pl.ANY)],
            out_specs=pl.BlockSpec(memory_space=pltpu.VMEM),
            scratch_shapes=scratch,
            compiler_params=pltpu.CompilerParams(collective_id=0, has_side_effects=True,
                                                 vmem_limit_bytes=60 * 1024 * 1024),
        )(lens, q, c)

    return jax.shard_map(local, mesh=mesh, in_specs=(P('dp', 'dcp', None), P('dp', None, 'dcp', None, None), P('dp')), out_specs=P('dp', 'dcp', None), check_vma=False)
```

time: 151 us -> 67.4 us (0.45)
  the two profiles are of different devices: /device:TPU:21 before, /device:TPU:28 now
where the time goes in v1:
time: 67.4 us; the launch traced here: 67.3 us
  Pallas kernels  65.7 us (97%)
  local copies, waits for them, and re-layouts  1.57 us (2%)
    pallas_call x1, Pallas kernels, local(): pl.pallas_call(functools.partial(kernel, n, page), out_shape=jax.ShapeDty...  65.7 us
    unnamed x1, local copies, waits for them, and re-layouts  1.57 us

profile of v1, /device:TPU:28, one launch (start us, length us, event | category | flops | bytes accessed | tf_op | source)
XLA Modules:
  0.0 67.3 jit_solution(3634122336564461691)
XLA Ops:
  0.0 65.7 %shard_map.37 = bf16[16,8,512]{2,1,0:T(8,128)(2,1)} custom-call(s32[16]{0:T(128)} %lens_ref.1, bf16[16,8,576]{2,1,0:T(8,128)(2,1)} %q_ref.1, bf16[16,8,576,128]{3,2,1,0:T(8,128)(2,1)} %bitcast.3), custom_call_target="tpu_custom_call" | custom-call | tf_op jit(solution)/shard_map/pallas_call | solution.py:314
  65.7 1.6 %copy.5 = bf16[16,8,512]{2,1,0:T(8,128)(2,1)} copy(bf16[16,8,512]{2,1,0:T(8,128)(2,1)} %shard_map.37) | data formatting | bytes 262144
